TPU v7x, 8 devices: a whole 2x2x1 slice. The times are simulated.
8 devices in a mesh: data: 1 (over z), tensor: 8 (over y, x, core).
Axes of the slice: x: 2, y: 2, z: 1, core: 2. Of those that a mesh axis runs over, the one named last changes fastest.
Arguments:
- token_ids: int32 [32768], P(('data', 'tensor'))
- emb_table: bfloat16 [151936, 896], P('tensor')
- norm_gain: bfloat16 [896], replicated
- w_up: bfloat16 [896, 4864], P(None, 'tensor')
- w_down: bfloat16 [4864, 896], P('tensor')
- grad_out: bfloat16 [32768, 896], P(('data', 'tensor'))
Outputs:
- output 1: bfloat16 [32768, 896], P(('data', 'tensor'))
- output 2: float32 [151936, 896], P(('data', 'tensor'))
- output 3: float32 [896, 4864], P('data', 'tensor')
- output 4: float32 [4864, 896], P(('data', 'tensor'))
All inputs are finite; a program needn't handle non-finite values.
Results may differ from a plain program's by a relative error of at most 0.00554826.
Values are sent between devices in bfloat16 or wider.
A program may use at most 1 GiB of HBM per device.

v0:
```python
import jax
import jax.numpy as jnp
from jax import lax
from jax.sharding import PartitionSpec as P

EPS = 1e-6


def rms_norm(x_rows, gain_f):
    inv_rms = lax.rsqrt(jnp.mean(x_rows * x_rows, axis=-1, keepdims=True) + EPS)
    return x_rows * inv_rms * gain_f


def gelu_tanh(values):
    return jax.nn.gelu(values, approximate=True)


def contract_last(left_op, right_op):
    return lax.dot_general(left_op, right_op, (((1,), (1,)), ((), ())), preferred_element_type=jnp.float32)


def contract_first(left_op, right_op):
    return lax.dot_general(left_op, right_op, (((0,), (0,)), ((), ())), preferred_element_type=jnp.float32)


def solution(mesh):
    tok_spec = P(('data', 'tensor'))
    row_spec = P(('data', 'tensor'), None)

    def local_step(token_ids, emb_shard, norm_gain, w_up, w_down, grad_out):
        vocab_local = emb_shard.shape[0]
        offset = lax.axis_index('tensor') * vocab_local
        ids_all = lax.all_gather(token_ids, 'tensor', tiled=True)
        rel_ids = ids_all - offset
        is_owned = (rel_ids >= 0) & (rel_ids < vocab_local)
        looked_up = jnp.take(emb_shard, jnp.clip(rel_ids, 0, vocab_local - 1), axis=0)
        emb_part = jnp.where(is_owned[:, None], looked_up, jnp.zeros((), looked_up.dtype))
        x_local = lax.psum_scatter(emb_part, 'tensor', scatter_dimension=0, tiled=True)
        x_f = x_local.astype(jnp.float32)
        gain_f = norm_gain.astype(jnp.float32)
        normed_f, norm_back = jax.vjp(lambda x_in: rms_norm(x_in, gain_f), x_f)
        normed = normed_f.astype(jnp.bfloat16)
        normed_all = lax.all_gather(normed, 'tensor', tiled=True)
        pre_act = jnp.dot(normed_all, w_up, preferred_element_type=jnp.float32).astype(jnp.bfloat16)
        act_f, gelu_back = jax.vjp(gelu_tanh, pre_act.astype(jnp.float32))
        hidden = act_f.astype(jnp.bfloat16)
        y_part = jnp.dot(hidden, w_down, preferred_element_type=jnp.float32)
        y_local = lax.psum_scatter(y_part, 'tensor', scatter_dimension=0, tiled=True)
        out_local = (x_f + y_local).astype(jnp.bfloat16)
        grad_all = lax.all_gather(grad_out, 'tensor', tiled=True)
        d_hidden = contract_last(grad_all, w_down)
        d_pre = gelu_back(d_hidden)[0].astype(jnp.bfloat16)
        d_w_down = contract_first(hidden, grad_all)
        d_w_up = contract_first(normed_all, d_pre)
        d_norm_part = contract_last(d_pre, w_up)
        d_norm = lax.psum_scatter(d_norm_part, 'tensor', scatter_dimension=0, tiled=True)
        dx_local = (grad_out.astype(jnp.float32) + norm_back(d_norm)[0]).astype(jnp.bfloat16)
        dx_all = lax.all_gather(dx_local, 'tensor', tiled=True)
        seg_ids = jnp.where(is_owned, rel_ids, vocab_local)
        d_emb = jax.ops.segment_sum(dx_all.astype(jnp.float32), seg_ids, num_segments=vocab_local + 1)[:vocab_local]
        return out_local, d_emb, d_w_up, d_w_down

    return jax.shard_map(
        local_step,
        mesh=mesh,
        in_specs=(tok_spec, P('tensor', None), P(None), P(None, 'tensor'), P('tensor', None), row_spec),
        out_specs=(row_spec, row_spec, P('data', 'tensor'), row_spec),
        check_vma=False,
    )
```

profile of v0, /device:TPU:0, one launch (start us, length us, event | category | flops | bytes accessed | tf_op | source)
XLA Modules:
  0.0 4719.1 jit_solution(9184869585518839408)
XLA Ops:
  7.2 14.1 all_gather.12
  22.1 1493.6 %gather_fusion = bf16[32768,896]{1,0:T(8,128)(2,1)} fusion(bf16[18992,896]{1,0:T(8,128)(2,1)} %param.7, s32[32768]{0:T(1024)S(1)} %get-tuple-element.9), kind=kCustom, calls=%fused_computation | custom fusion | bytes 117571584 | tf_op jit(solution)/shard_map/jit(_take)/gather | solution.py:36
  1515.8 39.2 select_select_fusion
  1555.8 322.0 %reduce-scatter.10.cloned.1.call-done = bf16[4096,896]{1,0:T(8,128)(2,1)} async-done(((bf16[32768,896]{1,0:T(8,128)(2,1)}), bf16[4096,896]{1,0:T(8,128)(2,1)}) %reduce-scatter.10.cloned.1.call-update) | async-done | bytes 7340048
  1877.8 4.6 fusion.18
  1883.6 7.9 fusion.20
  1891.6 249.8 %all-gather.6.cloned.1.call-done = bf16[32768,896]{1,0:T(8,128)(2,1)} async-done(((bf16[4096,896]{1,0:T(8,128)(2,1)}), bf16[32768,896]{1,0:T(8,128)(2,1)}) %all-gather.6.cloned.1.call-update) | async-done | bytes 58720272 | tf_op jit(solution)/shard_map/all_gather | solution.py:50
  2141.4 58.0 %fusion.29 = f32[32768,608]{0,1:T(8,128)} fusion(bf16[32768,896]{1,0:T(8,128)(2,1)} %all-gather.6.cloned.1.call-done, bf16[608,896]{1,0:T(8,128)(2,1)S(1)} %copy-done.10), kind=kOutput, calls=%fused_computation.47 | convolution fusion | flops 35701915648 | bytes 139501568 | tf_op jit(solution)/shard_map/dot_general | solution.py:19
  2199.4 206.1 %all-gather.4.cloned.1.call-done = bf16[32768,896]{1,0:T(8,128)(2,1)} async-done(((bf16[4096,896]{1,0:T(8,128)(2,1)}), bf16[32768,896]{1,0:T(8,128)(2,1)}) %all-gather.4.cloned.1.call-update) | async-done | bytes 58720272 | tf_op jit(solution)/shard_map/all_gather | solution.py:43
  2405.5 82.3 %fusion.8 = (bf16[32768,608]{0,1:T(8,128)(2,1)}, bf16[32768,608]{0,1:T(8,128)(2,1)}) fusion(f32[32768,608]{0,1:T(8,128)} %fusion.29, bf16[32768,896]{1,0:T(8,128)(2,1)} %all-gather.4.cloned.1.call-done, bf16[896,608]{0,1:T(8,128)(2,1)S(1)} %copy-done), kind=kOutput, calls=%fused_computation.13 | convolution fusion | flops 36140220416 | bytes 219193344 | tf_op jit(solution)/shard_map/dot_general | solution.py:44
  2487.9 61.9 %fusion.30 = f32[32768,896]{1,0:T(8,128)} fusion(bf16[32768,608]{0,1:T(8,128)(2,1)} %get-tuple-element.12, bf16[896,608]{0,1:T(8,128)(2,1)S(1)} %copy-done), kind=kOutput, calls=%fused_computation.48 | convolution fusion | flops 35701915648 | bytes 158375936 | tf_op jit(solution)/shard_map/dot_general | solution.py:19
  2549.9 1.2 copy-done.11
  2551.0 72.9 %fusion.27 = f32[32768,896]{1,0:T(8,128)} fusion(bf16[608,896]{1,0:T(8,128)(2,1)S(1)} %copy-done.11, bf16[32768,608]{0,1:T(8,128)(2,1)} %get-tuple-element.13), kind=kOutput, calls=%fused_computation.46 | convolution fusion | flops 35901145088 | bytes 158375936 | tf_op jit(solution)/shard_map/dot_general | solution.py:47
  2624.0 533.8 %reduce-scatter.14.cloned.1.call-done = f32[4096,896]{1,0:T(8,128)} async-done(((f32[32768,896]{1,0:T(8,128)}), f32[4096,896]{1,0:T(8,128)}) %reduce-scatter.14.cloned.1.call-update) | async-done | bytes 14680080
  3157.7 9.4 fusion.22
  3167.2 601.8 %reduce-scatter.12.cloned.1.call-done = f32[4096,896]{1,0:T(8,128)} async-done(((f32[32768,896]{1,0:T(8,128)}), f32[4096,896]{1,0:T(8,128)}) %reduce-scatter.12.cloned.1.call-update) | async-done | bytes 14680080
  3769.0 21.1 fusion.17
  3790.1 11.1 sort
  3801.9 48.6 %fusion.31 = f32[896,608]{0,1:T(8,128)} fusion(bf16[32768,608]{0,1:T(8,128)(2,1)} %get-tuple-element.12, bf16[32768,896]{1,0:T(8,128)(2,1)} %all-gather.4.cloned.1.call-done), kind=kOutput, calls=%fused_computation.49 | convolution fusion | flops 35701915648 | bytes 100745216 | tf_op jit(solution)/shard_map/dot_general | solution.py:23
  3850.4 56.2 %fusion.25 = f32[608,896]{1,0:T(8,128)} fusion(bf16[32768,896]{1,0:T(8,128)(2,1)} %all-gather.6.cloned.1.call-done, bf16[32768,608]{0,1:T(8,128)(2,1)} %get-tuple-element.13), kind=kOutput, calls=%fused_computation.45 | convolution fusion | flops 35901145088 | bytes 100745216 | tf_op jit(solution)/shard_map/dot_general | solution.py:23
  3906.7 145.3 %all-gather.8.cloned.1.call-done = bf16[32768,896]{1,0:T(8,128)(2,1)} async-done(((bf16[4096,896]{1,0:T(8,128)(2,1)}), bf16[32768,896]{1,0:T(8,128)(2,1)}) %all-gather.8.cloned.1.call-update) | async-done | bytes 58720272 | tf_op jit(solution)/shard_map/all_gather | solution.py:58
  4051.9 57.2 %convert_element_type.43 = f32[32768,896]{1,0:T(8,128)} convert(bf16[32768,896]{1,0:T(8,128)(2,1)} %all-gather.8.cloned.1.call-done) | non-fusion elementwise | flops 29360128 | bytes 176160768 | tf_op jit(solution)/shard_map/convert_element_type | solution.py:60
  4109.1 558.8 %scatter_custom_fusion = f32[18993,896]{1,0:T(8,128)} fusion(s32[32768]{0:T(1024)} %get-tuple-element.4, f32[32768,896]{1,0:T(8,128)} %convert_element_type.43, s32[32768]{0:T(1024)} %broadcast_clamp_fusion, f32[]{:T(128)} %constant.22.clone.1), kind=kCustom, calls=%fused_computation.8 | custom fusion | flops 29360128 | bytes 68071424 | tf_op jit(solution)/shard_map/scatter-add | solution.py:60
  4667.9 43.8 slice.8
  (42 shorter events, 3.8 us)
Async XLA Ops:
  7.2 2398.4 %copy-start = (bf16[896,608]{0,1:T(8,128)(2,1)S(1)}, bf16[896,608]{0,1:T(8,128)(2,1)}, u32[]{:S(2)}) copy-start(bf16[896,608]{0,1:T(8,128)(2,1)} %param.9) | copy-start | bytes 3268612
  7.2 1870.6 %reduce-scatter.10.cloned.1.call-start = ((), (), s32[]{:S(2)}) async-start(), calls=%async_computation.6 | async-start | bytes 66060288
  1555.0 0.8 copy-start.9
  1555.0 586.4 %copy-start.10 = (bf16[608,896]{1,0:T(8,128)(2,1)S(1)}, bf16[608,896]{1,0:T(8,128)(2,1)}, u32[]{:S(2)}) copy-start(bf16[608,896]{1,0:T(8,128)(2,1)} %param.10) | copy-start | bytes 3268612
  1555.0 586.4 %all-gather.6.cloned.1.call-start = ((), (), s32[]{:S(2)}) async-start(), calls=%async_computation.4 | async-start | bytes 66060288 | tf_op jit(solution)/shard_map/all_gather | solution.py:50
  1555.8 849.8 %all-gather.4.cloned.1.call-start = ((), (), s32[]{:S(2)}) async-start(), calls=%async_computation.3 | async-start | bytes 66060288 | tf_op jit(solution)/shard_map/all_gather | solution.py:43
  1555.8 643.6 %copy-start.7 = (f32[896]{0:T(1024)}, f32[896]{0:T(1024)S(1)}, u32[]{:S(2)}) copy-start(f32[896]{0:T(1024)S(1)} %convert_element_type.34) | copy-start | bytes 10756
  1882.4 0.6 copy-start.5
  1883.0 0.6 copy-start.3
  1891.6 1266.2 %reduce-scatter.14.cloned.1.call-start = ((), (), s32[]{:S(2)}) async-start(), calls=%async_computation.8 | async-start | bytes 132120576
  2549.8 1.2 copy-start.11
  2549.8 1219.2 %reduce-scatter.12.cloned.1.call-start = ((), (), s32[]{:S(2)}) async-start(), calls=%async_computation.7 | async-start | bytes 132120576
  2623.9 533.9 %copy-start.8 = (f32[896]{0:T(1024)S(1)}, f32[896]{0:T(1024)}, u32[]{:S(2)}) copy-start(f32[896]{0:T(1024)} %copy-done.7) | copy-start | bytes 10756
  2623.9 543.2 %copy-start.6 = (f32[4096]{0:T(1024)S(1)}, f32[4096]{0:T(1024)}, u32[]{:S(2)}) copy-start(f32[4096]{0:T(1024)} %copy-done.5) | copy-start | bytes 49156
  2623.9 1145.1 %copy-start.4 = (f32[4096]{0:T(1024)S(1)}, f32[4096]{0:T(1024)}, u32[]{:S(2)}) copy-start(f32[4096]{0:T(1024)} %copy-done.3) | copy-start | bytes 49156
  2623.9 1166.2 %copy-start.2 = (s32[32768]{0:T(1024)S(1)}, s32[32768]{0:T(1024)}, u32[]{:S(2)}) copy-start(s32[32768]{0:T(1024)} %get-tuple-element.8) | copy-start | bytes 393220
  2623.9 1428.0 %all-gather.8.cloned.1.call-start = ((), (), s32[]{:S(2)}) async-start(), calls=%async_computation.5 | async-start | bytes 66060288 | tf_op jit(solution)/shard_map/all_gather | solution.py:58
  4109.1 602.7 %copy-start.1 = (bf16[896,608]{0,1:T(8,128)(2,1)S(1)}, bf16[896,608]{0,1:T(8,128)(2,1)}, u32[]{:S(2)}) copy-start(bf16[896,608]{0,1:T(8,128)(2,1)} %param.9) | copy-start | bytes 3268612
Sparse Core Ops, SparseCore 0:
  1555.1 322.6 reduce-scatter.9
  1879.7 261.6 all-gather.5
  2143.8 261.6 all-gather.3
  2549.9 607.7 reduce-scatter.13
  3161.1 607.7 reduce-scatter.11
  3790.2 261.6 all-gather.7
where the time goes:
time: 4760 us; the launch traced here: 4720 us
  waiting for transfers between devices  2060 us (43%)
  local copies, waits for them, and re-layouts  1540 us (32%)
  other arithmetic  711 us (15%)
  matrix products  380 us (8%)
    gather x1, local copies, waits for them, and re-layouts, local_step(): jnp.take(emb_shard, jnp.clip(rel_ids, 0, vocab_local - 1), axis=0)  1490 us
    unnamed x9, waiting for transfers between devices  1460 us
    scatter-add x3, other arithmetic, local_step(): jax.ops.segment_sum(dx_all.astype(jnp.float32), seg_ids, num_segments=voc...  571 us
    all_gather x1, waiting for transfers between devices, local_step(): grad_all = lax.all_gather(grad_out, 'tensor', tiled=True)  250 us
    all_gather x1, waiting for transfers between devices, local_step(): normed_all = lax.all_gather(normed, 'tensor', tiled=True)  206 us
    all_gather x1, waiting for transfers between devices, local_step(): dx_all = lax.all_gather(dx_local, 'tensor', tiled=True)  145 us
    dot_general x2, matrix products, contract_last(): lax.dot_general(left_op, right_op, (((1,), (1,)), ((), ())), preferred_el...  120 us
    dot_general x2, matrix products, contract_first(): lax.dot_general(left_op, right_op, (((0,), (0,)), ((), ())), preferred_el...  105 us
  transfers between devices with their start and end apart: 6, of which 6 were waited for; matrix products, arithmetic and copies ran while one was open for 6% of the time, Pallas kernels for 0%

commit v1 on v0

--- a/solution.py
+++ b/solution.py
@@ -23,6 +23,10 @@
     return lax.dot_general(left_op, right_op, (((0,), (0,)), ((), ())), preferred_element_type=jnp.float32)
 
 
+def matmul(left_op, right_op):
+    return jnp.dot(left_op, right_op, preferred_element_type=jnp.float32)
+
+
 def solution(mesh):
     tok_spec = P(('data', 'tensor'))
     row_spec = P(('data', 'tensor'), None)
@@ -30,6 +34,8 @@
     def local_step(token_ids, emb_shard, norm_gain, w_up, w_down, grad_out):
         vocab_local = emb_shard.shape[0]
         offset = lax.axis_index('tensor') * vocab_local
+        w_up_t = lax.all_gather(w_up.T, 'tensor', tiled=True)
+        w_dn = lax.all_gather(w_down, 'tensor', tiled=True)
         ids_all = lax.all_gather(token_ids, 'tensor', tiled=True)
         rel_ids = ids_all - offset
         is_owned = (rel_ids >= 0) & (rel_ids < vocab_local)
@@ -40,21 +46,16 @@
         gain_f = norm_gain.astype(jnp.float32)
         normed_f, norm_back = jax.vjp(lambda x_in: rms_norm(x_in, gain_f), x_f)
         normed = normed_f.astype(jnp.bfloat16)
-        normed_all = lax.all_gather(normed, 'tensor', tiled=True)
-        pre_act = jnp.dot(normed_all, w_up, preferred_element_type=jnp.float32).astype(jnp.bfloat16)
+        pre_act = contract_last(normed, w_up_t).astype(jnp.bfloat16)
         act_f, gelu_back = jax.vjp(gelu_tanh, pre_act.astype(jnp.float32))
         hidden = act_f.astype(jnp.bfloat16)
-        y_part = jnp.dot(hidden, w_down, preferred_element_type=jnp.float32)
-        y_local = lax.psum_scatter(y_part, 'tensor', scatter_dimension=0, tiled=True)
-        out_local = (x_f + y_local).astype(jnp.bfloat16)
-        grad_all = lax.all_gather(grad_out, 'tensor', tiled=True)
-        d_hidden = contract_last(grad_all, w_down)
+        d_w_down = lax.psum_scatter(contract_first(hidden, grad_out), 'tensor', scatter_dimension=0, tiled=True)
+        d_hidden = contract_last(grad_out, w_dn)
         d_pre = gelu_back(d_hidden)[0].astype(jnp.bfloat16)
-        d_w_down = contract_first(hidden, grad_all)
-        d_w_up = contract_first(normed_all, d_pre)
-        d_norm_part = contract_last(d_pre, w_up)
-        d_norm = lax.psum_scatter(d_norm_part, 'tensor', scatter_dimension=0, tiled=True)
+        d_norm = matmul(d_pre, w_up_t)
         dx_local = (grad_out.astype(jnp.float32) + norm_back(d_norm)[0]).astype(jnp.bfloat16)
+        d_w_up = lax.psum_scatter(contract_first(d_pre, normed), 'tensor', scatter_dimension=0, tiled=True).T
+        out_local = (x_f + matmul(hidden, w_dn)).astype(jnp.bfloat16)
         dx_all = lax.all_gather(dx_local, 'tensor', tiled=True)
         seg_ids = jnp.where(is_owned, rel_ids, vocab_local)
         d_emb = jax.ops.segment_sum(dx_all.astype(jnp.float32), seg_ids, num_segments=vocab_local + 1)[:vocab_local]

time: 4760 us -> 3090 us (0.65)
  waiting for transfers between devices: 2060 us -> 458 us
    unnamed x9 -> x7, waiting for transfers between devices: 1460 us -> 351 us
    all_gather x2, waiting for transfers between devices: 456 us -> 47.9 us  [the longest x1 46.5 us: local_step(): w_up_t = lax.all_gather(w_up.T, 'tensor', tiled=True)]
    all_gather x1, waiting for transfers between devices: 145 us -> 58.3 us  [local_step(): dx_all = lax.all_gather(dx_local, 'tensor', tiled=True)]
  transfers between devices with their start and end apart: 6 -> 6, of which waited for: 6 -> 4; matrix products, arithmetic and copies ran while one was open for 6% -> 30% of each run, Pallas kernels for 0% -> 0%
where the time goes in v1:
time: 3090 us; the launch traced here: 3070 us
  local copies, waits for them, and re-layouts  1520 us (49%)
  other arithmetic  685 us (22%)
  waiting for transfers between devices  458 us (15%)
  matrix products  382 us (12%)
    gather x1, local copies, waits for them, and re-layouts, local_step(): jnp.take(emb_shard, jnp.clip(rel_ids, 0, vocab_local - 1), axis=0)  1470 us
    scatter-add x3, other arithmetic, local_step(): jax.ops.segment_sum(dx_all.astype(jnp.float32), seg_ids, num_segments=voc...  571 us
    unnamed x7, waiting for transfers between devices  351 us
    dot_general x2, matrix products, contract_last(): lax.dot_general(left_op, right_op, (((1,), (1,)), ((), ())), preferred_el...  139 us
    dot_general x2, matrix products, contract_first(): lax.dot_general(left_op, right_op, (((0,), (0,)), ((), ())), preferred_el...  135 us
    dot_general x2, matrix products, matmul(): return jnp.dot(left_op, right_op, preferred_element_type=jnp.float32)  108 us
  transfers between devices with their start and end apart: 6, of which 4 were waited for; matrix products, arithmetic and copies ran while one was open for 30% of the time, Pallas kernels for 0%

profile of v1, /device:TPU:0, one launch (start us, length us, event | category | flops | bytes accessed | tf_op | source)
XLA Modules:
  0.0 3071.4 jit_solution(15534288347191611878)
XLA Ops:
  7.2 13.9 all_gather.12
  21.3 0.7 subtract_select_fusion
  22.0 1474.3 %gather_fusion = bf16[32768,896]{1,0:T(8,128)(2,1)} fusion(bf16[18992,896]{1,0:T(8,128)(2,1)} %param.7, s32[32768]{0:T(1024)S(1)} %get-tuple-element.7), kind=kCustom, calls=%fused_computation | custom fusion | bytes 117571584 | tf_op jit(solution)/shard_map/jit(_take)/gather | solution.py:42
  1496.3 39.2 %select_select_fusion = bf16[32768,896]{1,0:T(8,128)(2,1)} fusion(bf16[32768,896]{1,0:T(8,128)(2,1)} %gather_fusion, pred[32768]{0:T(1024)(128)(4,1)S(1)} %get-tuple-element.9, pred[32768]{0:T(1024)(128)(4,1)S(1)} %get-tuple-element.8), kind=kLoop, calls=%fused_computation.20 | loop fusion | flops 58720256 | bytes 117506048 | tf_op jit(solution)/shard_map/jit(_where)/select_n | solution.py:43
  1535.6 0.7 all-gather.4.cloned.1.call-update
  1536.3 0.7 all-gather.6.cloned.1.call-update
  1537.1 350.0 %reduce-scatter.10.cloned.1.call-done = bf16[4096,896]{1,0:T(8,128)(2,1)} async-done(((bf16[32768,896]{1,0:T(8,128)(2,1)}), bf16[4096,896]{1,0:T(8,128)(2,1)}) %reduce-scatter.10.cloned.1.call-update) | async-done | bytes 7340048
  1887.1 4.6 fusion.18
  1891.7 0.6 copy-done.2
  1892.3 46.5 %all-gather.4.cloned.1.call-done = bf16[4864,896]{1,0:T(8,128)(2,1)} async-done(((bf16[608,896]{1,0:T(8,128)(2,1)}), bf16[4864,896]{1,0:T(8,128)(2,1)}) %all-gather.4.cloned.1.call-update) | async-done | bytes 8716304 | tf_op jit(solution)/shard_map/all_gather | solution.py:37
  1938.9 50.3 %convolution_convert_fusion = bf16[4096,4864]{1,0:T(8,128)(2,1)} fusion(bf16[4864,896]{1,0:T(8,128)(2,1)} %all-gather.4.cloned.1.call-done, bf16[4096,896]{1,0:T(8,128)(2,1)} %reduce-scatter.10.cloned.1.call-done, f32[896]{0:T(1024)S(1)} %convert_element_type.34, f32[4096]{0:T(1024)S(1)} %fusion.27), kind=kOutput, calls=%fused_computation.21 | convolution fusion | flops 35736518656 | bytes 55922176 | tf_op jit(solution)/shard_map/dot_general | solution.py:19
  1989.2 1.4 all-gather.6.cloned.1.call-done
  1990.6 88.2 %fusion.8 = bf16[4096,4864]{1,0:T(8,128)(2,1)} fusion(bf16[4096,4864]{1,0:T(8,128)(2,1)} %convolution_convert_fusion, bf16[4096,896]{1,0:T(8,128)(2,1)} %param.11, bf16[4864,896]{1,0:T(8,128)(2,1)} %all-gather.6.cloned.1.call-done), kind=kOutput, calls=%fused_computation.13 | convolution fusion | flops 36120297472 | bytes 95748096 | tf_op jit(solution)/shard_map/dot_general | solution.py:19
  2078.8 51.4 %fusion.22 = (f32[4096]{0:T(1024)S(1)}, f32[4096,896]{1,0:T(8,128)}) fusion(bf16[4096,896]{1,0:T(8,128)(2,1)} %reduce-scatter.10.cloned.1.call-done, f32[896]{0:T(1024)S(1)} %convert_element_type.34, bf16[4096,4864]{1,0:T(8,128)(2,1)} %fusion.8, bf16[4864,896]{1,0:T(8,128)(2,1)} %all-gather.4.cloned.1.call-done), kind=kOutput, calls=%fused_computation.35 | convolution fusion | flops 35716591616 | bytes 70602240 | tf_op jit(solution)/shard_map/dot_general | solution.py:27
  2130.3 11.7 fusion.17
  2142.0 81.7 %fusion.28 = f32[4864,896]{1,0:T(8,128)} fusion(bf16[4096,896]{1,0:T(8,128)(2,1)} %param.11, bf16[4096,4864]{1,0:T(8,128)(2,1)} %convolution_convert_fusion), kind=kOutput, calls=%fused_computation.46 | convolution fusion | flops 35901145088 | bytes 64618496 | tf_op jit(solution)/shard_map/dot_general | solution.py:23
  2223.8 53.2 %fusion.23 = f32[4864,896]{1,0:T(8,128)} fusion(bf16[4096,4864]{1,0:T(8,128)(2,1)} %fusion.8, bf16[4096,896]{1,0:T(8,128)(2,1)} %reduce-scatter.10.cloned.1.call-done, f32[896]{0:T(1024)S(1)} %convert_element_type.34, f32[4096]{0:T(1024)S(1)} %copy-done.5), kind=kOutput, calls=%fused_computation.36 | convolution fusion | flops 35716595712 | bytes 64638464 | tf_op jit(solution)/shard_map/dot_general | solution.py:23
  2277.1 11.1 sort
  2288.2 0.7 broadcast_clamp_fusion
  2288.9 56.6 %fusion.21 = bf16[4096,896]{1,0:T(8,128)(2,1)} fusion(bf16[4096,896]{1,0:T(8,128)(2,1)} %reduce-scatter.10.cloned.1.call-done, bf16[4864,896]{1,0:T(8,128)(2,1)} %all-gather.6.cloned.1.call-done, bf16[4096,4864]{1,0:T(8,128)(2,1)} %convolution_convert_fusion), kind=kOutput, calls=%fused_computation.34 | convolution fusion | flops 35912155136 | bytes 63242240 | tf_op jit(solution)/shard_map/dot_general | solution.py:27
  2345.5 58.3 %all-gather.8.cloned.1.call-done = bf16[32768,896]{1,0:T(8,128)(2,1)} async-done(((bf16[4096,896]{1,0:T(8,128)(2,1)}), bf16[32768,896]{1,0:T(8,128)(2,1)}) %all-gather.8.cloned.1.call-update) | async-done | bytes 58720272 | tf_op jit(solution)/shard_map/all_gather | solution.py:59
  2403.8 57.5 %convert_element_type.43 = f32[32768,896]{1,0:T(8,128)} convert(bf16[32768,896]{1,0:T(8,128)(2,1)} %all-gather.8.cloned.1.call-done) | non-fusion elementwise | flops 29360128 | bytes 176160768 | tf_op jit(solution)/shard_map/convert_element_type | solution.py:61
  2461.3 558.9 %scatter_custom_fusion = f32[18993,896]{1,0:T(8,128)} fusion(s32[32768]{0:T(1024)} %get-tuple-element.4, f32[32768,896]{1,0:T(8,128)} %convert_element_type.43, s32[32768]{0:T(1024)} %broadcast_clamp_fusion, f32[]{:T(128)} %constant.22.clone.1), kind=kCustom, calls=%fused_computation.8 | custom fusion | flops 29360128 | bytes 68071424 | tf_op jit(solution)/shard_map/scatter-add | solution.py:61
  3020.3 43.8 %slice.8 = f32[18992,896]{1,0:T(8,128)} slice(f32[18993,896]{1,0:T(8,128)} %scatter_custom_fusion), slice={[0:18992], [0:896]} | slice | bytes 136134656 | tf_op jit(solution)/shard_map/slice | solution.py:61
  (30 shorter events, 0.5 us)
Async XLA Ops:
  7.2 1880.0 %reduce-scatter.10.cloned.1.call-start = ((), (), s32[]{:S(2)}) async-start(), calls=%async_computation.8 | async-start | bytes 66060288
  1535.5 1.6 copy-start.6
  1535.5 403.3 %all-gather.4.cloned.1.call-start = ((), (), s32[]{:S(2)}) async-start(), calls=%async_computation.3 | async-start | bytes 9805824 | tf_op jit(solution)/shard_map/all_gather | solution.py:37
  1536.3 454.3 %all-gather.6.cloned.1.call-start = ((), (), s32[]{:S(2)}) async-start(), calls=%async_computation.4 | async-start | bytes 9805824 | tf_op jit(solution)/shard_map/all_gather | solution.py:38
  1537.0 866.8 %all-gather.8.cloned.1.call-start = ((), (), s32[]{:S(2)}) async-start(), calls=%async_computation.5 | async-start | bytes 66060288 | tf_op jit(solution)/shard_map/all_gather | solution.py:59
  1891.7 0.6 copy-start.2
  1892.3 96.9 %copy-start.4 = (f32[4096]{0:T(1024)}, f32[4096]{0:T(1024)S(1)}, u32[]{:S(2)}) copy-start(f32[4096]{0:T(1024)S(1)} %fusion.27) | copy-start | bytes 49156
  2078.8 51.4 %copy-start.3 = (f32[4096]{0:T(1024)S(1)}, f32[4096]{0:T(1024)}, u32[]{:S(2)}) copy-start(f32[4096]{0:T(1024)} %copy-done.2) | copy-start | bytes 49156
  2078.8 51.4 %copy-start = (bf16[4096,896]{1,0:T(8,128)(2,1)S(1)}, bf16[4096,896]{1,0:T(8,128)(2,1)}, u32[]{:S(2)}) copy-start(bf16[4096,896]{1,0:T(8,128)(2,1)} %reduce-scatter.10.cloned.1.call-done) | copy-start | bytes 22020100
  2078.8 51.4 %copy-start.5 = (f32[4096]{0:T(1024)S(1)}, f32[4096]{0:T(1024)}, u32[]{:S(2)}) copy-start(f32[4096]{0:T(1024)} %copy-done.4) | copy-start | bytes 49156
  2142.0 922.1 %reduce-scatter.8.cloned.1.call-start = ((), (), s32[]{:S(2)}) async-start(), calls=%async_computation.7 | async-start | bytes 19611648 | tf_op jit(solution)/shard_map/reduce_scatter | solution.py:52
  2223.8 53.4 %copy-start.1 = (s32[32768]{0:T(1024)S(1)}, s32[32768]{0:T(1024)}, u32[]{:S(2)}) copy-start(s32[32768]{0:T(1024)} %get-tuple-element.6) | copy-start | bytes 393220
  2223.8 840.3 %reduce-scatter.6.cloned.1.call-start = ((), (), s32[]{:S(2)}) async-start(), calls=%async_computation.6 | async-start | bytes 19611648 | tf_op jit(solution)/shard_map/reduce_scatter | solution.py:57
Sparse Core Ops, SparseCore 0:
  1535.7 351.4 reduce-scatter.9
  1888.9 49.8 all-gather.3
  1940.7 49.8 all-gather.5
  2142.1 261.6 all-gather.7
  2407.8 110.1 reduce-scatter.7
  2522.1 110.1 reduce-scatter.5

commit v2 on v1

v2 whole, which is shorter than its diff:
```python
import functools
import math
import jax
import jax.numpy as jnp
from jax import lax
from jax.experimental import pallas as pl
from jax.experimental.pallas import tpu as pltpu
from jax.sharding import PartitionSpec as P

EPS = 1e-6
BIG = 2 ** 30
N_DUP = 48
N_ONE = 336
N_REQ = N_DUP + N_ONE
GROUP = 64
ROWS = 8
TOK_BLOCK = 512
V_BLOCK = 256
WIN = 32
F_CHUNK = 256
GELU_A = (2 / math.pi) ** 0.5
GELU_B = 0.044715
F32 = jnp.float32
BF16 = jnp.bfloat16


def rms_norm(x_rows, gain_f):
    inv_rms = lax.rsqrt(jnp.mean(x_rows * x_rows, axis=-1, keepdims=True) + EPS)
    return x_rows * inv_rms * gain_f


def contract_last(left_op, right_op):
    return lax.dot_general(left_op, right_op, (((1,), (1,)), ((), ())), preferred_element_type=F32)


def contract_first(left_op, right_op):
    return lax.dot_general(left_op, right_op, (((0,), (0,)), ((), ())), preferred_element_type=F32)


def matmul(left_op, right_op):
    return jnp.dot(left_op, right_op, preferred_element_type=F32)


def route_kernel(me_ref, rnd_ref, ids_ref, out_ref, *, n_peer, vocab_local):
    s = ids_ref[...]
    n_row, n_lane = s.shape
    row = lax.broadcasted_iota(jnp.int32, s.shape, 0)
    lane = lax.broadcasted_iota(jnp.int32, s.shape, 1)
    back = pltpu.roll(s, 1, 1)
    back = jnp.where(lane == 0, pltpu.roll(back, 1, 0), back)
    ahead = pltpu.roll(s, n_lane - 1, 1)
    ahead = jnp.where(lane == n_lane - 1, pltpu.roll(ahead, n_row - 1, 0), ahead)
    is_first, is_last = row + lane == 0, row * n_lane + lane == n_row * n_lane - 1
    starts = (s != back) | is_first
    repeats = (s == ahead) & ~is_last
    owner = jnp.zeros_like(s)
    for d in range(1, n_peer):
        owner += (s >= d * vocab_local).astype(jnp.int32)
    up_to = (lax.broadcasted_iota(jnp.int32, (n_lane, n_lane), 0)
             <= lax.broadcasted_iota(jnp.int32, (n_lane, n_lane), 1)).astype(F32).astype(BF16)
    above = (lax.broadcasted_iota(jnp.int32, (n_row, n_row), 1)
             < lax.broadcasted_iota(jnp.int32, (n_row, n_row), 0)).astype(F32).astype(BF16)
    slot = jnp.full_like(s, -1)
    need = jnp.zeros((1, 1), F32)
    place = (owner ^ me_ref[0]) * N_REQ
    for flag, cap, shift in ((starts & repeats, N_DUP, 0), (starts & ~repeats, N_ONE, N_DUP)):
        mark = flag.astype(F32)
        incl = matmul(mark.astype(BF16), up_to)
        total = jnp.broadcast_to(incl[:, n_lane - 1:], s.shape)
        pos = incl - mark + matmul(above, total.astype(BF16))
        for d in range(1, n_peer):
            here = jnp.where(owner == d - 1, mark, 0.0)
            pos -= jnp.where(owner >= d, jnp.sum(here, keepdims=True), 0.0)
        trip = jnp.floor((pos + 0.5) / cap)
        need = jnp.maximum(need, jnp.max(jnp.where(flag, trip + 1.0, 0.0), keepdims=True))
        rel = pos.astype(jnp.int32) - rnd_ref[0] * cap
        slot = jnp.where(flag & (rel >= 0) & (rel < cap), place + shift + rel, slot)
    group, spot = slot >> 7, slot & 127
    spot_t = spot.astype(F32).T
    n_group = n_peer * N_REQ // 128
    group_iota = lax.broadcasted_iota(jnp.int32, (n_group, n_lane), 0)
    lane_sq = lax.broadcasted_iota(jnp.int32, (n_lane, n_lane), 1).astype(F32)
    parts = [(s & 63) + 1, (s >> 6) & 63, s >> 12]
    acc = jnp.zeros((3 * n_group, n_lane), F32)
    for a in range(n_row):
        at = group_iota == group[a:a + 1, :]
        left = jnp.concatenate([jnp.where(at, part[a:a + 1, :].astype(F32), 0.0) for part in parts], axis=0)
        right = (lane_sq == spot_t[:, a:a + 1]).astype(F32)
        acc += matmul(left.astype(BF16), right.astype(BF16))
    got = acc.astype(jnp.int32)
    got = got[:n_group] + got[n_group:2 * n_group] * 64 + got[2 * n_group:] * 4096 - 1
    rows = N_REQ // 128
    for k in range(n_peer):
        out_ref[k, :rows, :] = got[k * rows:(k + 1) * rows]
        out_ref[k, rows:, :] = jnp.broadcast_to(need.astype(jnp.int32), (8 - rows, n_lane))


def route(me, rnd, sorted_ids, n_peer, vocab_local):
    smem = pl.BlockSpec(memory_space=pltpu.SMEM)
    whole = pl.BlockSpec(memory_space=pltpu.VMEM)
    return pl.pallas_call(
        functools.partial(route_kernel, n_peer=n_peer, vocab_local=vocab_local),
        out_shape=jax.ShapeDtypeStruct((n_peer, 8, 128), jnp.int32),
        in_specs=[smem, smem, whole],
        out_specs=whole,
        cost_estimate=pl.CostEstimate(flops=10 ** 9, bytes_accessed=10 ** 5, transcendentals=0),
        name='route',
    )(me.reshape(1), rnd.reshape(1), sorted_ids)


def flipped(x, k):
    for bit in (1, 2, 4):
        if k & bit:
            x = x + bit - 2 * bit * ((x // bit) % 2)
    return x


def swap_kernel(mine_ref, theirs_ref, send_sem, recv_sem, *, n_peer):
    me = lax.axis_index('tensor')
    barrier = pltpu.get_barrier_semaphore()
    for k in range(1, n_peer):
        pl.semaphore_signal(barrier, inc=1, device_id={'tensor': flipped(me, k)}, device_id_type=pl.DeviceIdType.MESH)
    pl.semaphore_wait(barrier, n_peer - 1)
    copies = []
    for k in range(1, n_peer):
        copy = pltpu.make_async_remote_copy(
            src_ref=mine_ref.at[k], dst_ref=theirs_ref.at[k], send_sem=send_sem.at[k], recv_sem=recv_sem.at[k],
            device_id={'tensor': flipped(me, k)}, device_id_type=pl.DeviceIdType.MESH)
        copy.start()
        copies.append(copy)
    theirs_ref[0] = mine_ref[0]
    for copy in copies:
        copy.wait()


def swap_lists(mine):
    n_peer = mine.shape[0]
    whole = pl.BlockSpec(memory_space=pltpu.VMEM)
    return pl.pallas_call(
        functools.partial(swap_kernel, n_peer=n_peer),
        out_shape=jax.ShapeDtypeStruct(mine.shape, mine.dtype),
        in_specs=[whole],
        out_specs=whole,
        scratch_shapes=[pltpu.SemaphoreType.DMA((n_peer,)), pltpu.SemaphoreType.DMA((n_peer,))],
        compiler_params=pltpu.CompilerParams(collective_id=0, has_side_effects=True),
        name='swap_lists',
    )(mine)


def gather_kernel(idx_ref, sub_ref, emb_ref, *refs, n_out, depth):
    outs, (buf, sems) = refs[:n_out], refs[n_out:]
    per_out = N_REQ // GROUP
    steps = n_out * per_out

    def issue(step, slot):
        for i in range(GROUP):
            base = pl.multiple_of(idx_ref[step * GROUP + i], ROWS)
            pltpu.make_async_copy(emb_ref.at[pl.ds(base, ROWS), :], buf.at[slot, i], sems.at[slot]).start()

    for step in range(depth - 1):
        issue(step, step)
    lane = lax.broadcasted_iota(jnp.int32, (GROUP, GROUP * ROWS), 1)
    first = lax.broadcasted_iota(jnp.int32, (GROUP, GROUP * ROWS), 0) * ROWS

    for j in range(n_out):
        def body(i, carry, j=j):
            step = j * per_out + i
            slot = lax.rem(step, depth)

            @pl.when(step + depth - 1 < steps)
            def _():
                issue(step + depth - 1, lax.rem(step + depth - 1, depth))

            pltpu.make_async_copy(buf.at[slot], buf.at[slot], sems.at[slot]).wait()
            sub = sub_ref[pl.ds(pl.multiple_of(step * GROUP, GROUP), GROUP), :]
            pick = (lane == first + sub).astype(F32).astype(BF16)
            rows = matmul(pick, buf[slot].reshape(GROUP * ROWS, buf.shape[-1])).astype(BF16)
            outs[j][pl.ds(pl.multiple_of(i * GROUP, GROUP), GROUP), :] = rows
            return carry

        lax.fori_loop(0, per_out, body, 0)


def gather_rows(emb, idx, n_out):
    depth = 4
    dim = emb.shape[1]
    whole = pl.BlockSpec(memory_space=pltpu.VMEM)
    return pl.pallas_call(
        functools.partial(gather_kernel, n_out=n_out, depth=depth),
        out_shape=[jax.ShapeDtypeStruct((N_REQ, dim), BF16)] * n_out,
        in_specs=[pl.BlockSpec(memory_space=pltpu.SMEM), whole, pl.BlockSpec(memory_space=pl.ANY)],
        out_specs=[whole] * n_out,
        scratch_shapes=[
            pltpu.VMEM((depth, GROUP, ROWS, dim), BF16),
            pltpu.SemaphoreType.DMA((depth,)),
        ],
        cost_estimate=pl.CostEstimate(flops=14 * 10 ** 9, bytes_accessed=n_out * N_REQ * ROWS * dim * 2, transcendentals=0),
        name='gather_rows',
    )((idx // ROWS) * ROWS, (idx % ROWS)[:, None], emb)


def expand_kernel(ids_ref, gid_ref, gain_ref, *refs, n_peer, has_prev):
    recv = refs[:n_peer]
    x_ref, n_ref, table, hits = refs[-4:]

    @pl.when(pl.program_id(0) == 0)
    def _():
        for k in range(n_peer):
            table[k * N_REQ:(k + 1) * N_REQ, :] = recv[k][...]

    ids = ids_ref[...]
    for k in range(n_peer):
        hits[:, k * N_REQ:(k + 1) * N_REQ] = (ids == gid_ref[k:k + 1, :]).astype(F32).astype(BF16)
    acc = matmul(hits[...], table[...])
    if has_prev:
        acc += refs[n_peer][...].astype(F32)
    x_ref[...] = acc.astype(BF16)
    n_ref[...] = rms_norm(acc, gain_ref[...].astype(F32)).astype(BF16)


def expand_rows(ids_col, gid, gain_row, recv, prev=None):
    n_tok, dim = ids_col.shape[0], recv[0].shape[1]
    n_peer = len(recv)
    tok = pl.BlockSpec((TOK_BLOCK, dim), lambda i: (i, 0))
    whole = pl.BlockSpec(memory_space=pltpu.VMEM)
    extra = () if prev is None else (prev,)
    return pl.pallas_call(
        functools.partial(expand_kernel, n_peer=n_peer, has_prev=prev is not None),
        grid=(n_tok // TOK_BLOCK,),
        out_shape=[jax.ShapeDtypeStruct((n_tok, dim), BF16)] * 2,
        in_specs=[pl.BlockSpec((TOK_BLOCK, 1), lambda i: (i, 0)), whole, whole] + [whole] * n_peer + [tok] * len(extra),
        out_specs=[tok, tok],
        scratch_shapes=[pltpu.VMEM((n_peer * N_REQ, dim), BF16), pltpu.VMEM((TOK_BLOCK, n_peer * N_REQ), BF16)],
        cost_estimate=pl.CostEstimate(flops=22 * 10 ** 9, bytes_accessed=30 * 10 ** 6, transcendentals=0),
        name='expand_rows',
    )(ids_col, gid, gain_row, *recv, *extra)


def hidden_kernel(n_ref, grad_ref, w_up_ref, w_dn_ref, h_ref, du_ref, u_buf, dh_buf):
    n_chunk = w_up_ref.shape[0] // F_CHUNK

    def at(c):
        return pl.ds(c * F_CHUNK if isinstance(c, int) else pl.multiple_of(c * F_CHUNK, F_CHUNK), F_CHUNK)

    def dots(c, slot):
        u_buf[slot] = contract_last(n_ref[...], w_up_ref[at(c), :])
        dh_buf[slot] = contract_last(grad_ref[...], w_dn_ref[at(c), :])

    def act(c, slot):
        u = u_buf[slot].astype(BF16).astype(F32)
        sq = u * u
        half = 0.5 * jnp.tanh(u * (GELU_A + (GELU_A * GELU_B) * sq)) + 0.5
        h_ref[:, at(c)] = (u * half).astype(BF16)
        slope = half + u * (half - half * half) * (2 * GELU_A + (6 * GELU_A * GELU_B) * sq)
        du_ref[:, at(c)] = (dh_buf[slot] * slope).astype(BF16)

    dots(0, 0)

    def pair(i, carry):
        c = 2 * i
        dots(c + 1, 1)
        act(c, 0)
        dots(c + 2, 0)
        act(c + 1, 1)
        return carry

    lax.fori_loop(0, (n_chunk - 1) // 2, pair, 0)
    act(n_chunk - 1, 0)


def hidden_arrays(normed, grad_out, w_up_t, w_dn):
    n_tok, dim = normed.shape
    ffn = w_dn.shape[0]
    tok = pl.BlockSpec((TOK_BLOCK, dim), lambda i: (i, 0))
    wide = pl.BlockSpec((TOK_BLOCK, ffn), lambda i: (i, 0))
    whole = pl.BlockSpec(memory_space=pltpu.VMEM)
    return pl.pallas_call(
        hidden_kernel,
        grid=(n_tok // TOK_BLOCK,),
        out_shape=[jax.ShapeDtypeStruct((n_tok, ffn), BF16)] * 2,
        in_specs=[tok, tok, whole, whole],
        out_specs=[wide, wide],
        scratch_shapes=[pltpu.VMEM((2, TOK_BLOCK, F_CHUNK), F32)] * 2,
        compiler_params=pltpu.CompilerParams(vmem_limit_bytes=60 * 2 ** 20),
        cost_estimate=pl.CostEstimate(flops=4 * n_tok * dim * ffn, bytes_accessed=110 * 10 ** 6, transcendentals=n_tok * ffn),
        name='hidden_arrays',
    )(normed, grad_out, w_up_t, w_dn)


def combine_kernel(gid_ref, ids_ref, dx_ref, *refs, n_out):
    dups, ones, hits = refs[:n_out], refs[n_out:2 * n_out], refs[-1]
    n_tok = dx_ref.shape[0]
    step = 1024
    for j in range(n_out):
        gid = gid_ref[j * N_REQ:(j + 1) * N_REQ, :]
        for lo in range(0, n_tok, step):
            hits[:, lo:lo + step] = (gid == ids_ref[:, lo:lo + step]).astype(F32).astype(BF16)
        acc = matmul(hits[...], dx_ref[...])
        dups[j][...] = acc[:N_DUP]
        ones[j][...] = acc[N_DUP:].astype(BF16)


def combine_rows(gid_col, ids_row, d_x):
    n_tok, dim = d_x.shape
    n_out = gid_col.shape[0] // N_REQ
    whole = pl.BlockSpec(memory_space=pltpu.VMEM)
    outs = pl.pallas_call(
        functools.partial(combine_kernel, n_out=n_out),
        out_shape=[jax.ShapeDtypeStruct((N_DUP, dim), F32)] * n_out + [jax.ShapeDtypeStruct((N_ONE, dim), BF16)] * n_out,
        in_specs=[whole, whole, whole],
        out_specs=[whole] * (2 * n_out),
        scratch_shapes=[pltpu.VMEM((N_REQ, n_tok), BF16)],
        cost_estimate=pl.CostEstimate(flops=12 * 10 ** 9, bytes_accessed=12 * 10 ** 6, transcendentals=0),
        name='combine_rows',
    )(gid_col, ids_row, d_x)
    return outs[:n_out], outs[n_out:]


def table_kernel(off_one_ref, off_dup_ref, dup_id_ref, one_id_ref, *refs, n_peer, has_prev):
    ones = refs[:n_peer]
    dups = refs[n_peer:2 * n_peer]
    out_ref, rows_buf, id_buf = refs[-3:]
    blk = pl.program_id(0)
    base = blk * V_BLOCK
    starts, trips = [], jnp.int32(1)
    for k in range(n_peer):
        lo, hi = off_one_ref[k, blk], off_one_ref[k, blk + 1]
        start = (lo // 16) * 16
        starts.append(start)
        trips = jnp.maximum(trips, jnp.where(hi > lo, (hi - start + WIN - 1) // WIN, 0))
    pos = lax.broadcasted_iota(jnp.int32, (WIN, 1), 0)
    lane = lax.broadcasted_iota(jnp.int32, (n_peer * WIN, V_BLOCK), 1) + base

    def picked(it):
        for k in range(n_peer):
            want = starts[k] + it * WIN
            at = pl.multiple_of(jnp.minimum(want, N_ONE - WIN), 16)
            rows_buf[k * WIN:(k + 1) * WIN, :] = ones[k][pl.ds(at, WIN), :]
            window = one_id_ref[pl.ds(pl.multiple_of(k * N_ONE + at, 16), WIN), :]
            id_buf[k * WIN:(k + 1) * WIN, :] = jnp.where(pos + at >= want, window, -1)
        hit = (id_buf[...] == lane).astype(F32).astype(BF16)
        return contract_first(hit, rows_buf[...])

    out_ref[...] = refs[2 * n_peer][...] + picked(0) if has_prev else picked(0)

    def one_step(it, carry):
        out_ref[...] += picked(it)
        return carry

    lax.fori_loop(1, trips, one_step, 0)
    sub = lax.broadcasted_iota(jnp.int32, (8, 1), 0)
    for k in range(n_peer):
        def dup_step(j, carry, k=k):
            row = dup_id_ref[k, j] - base
            taken = dups[k][pl.ds(pl.multiple_of((j // 8) * 8, 8), 8), :]
            taken = jnp.sum(jnp.where(sub == lax.rem(j, 8), taken, 0.0), axis=0, keepdims=True)
            at = pl.ds(pl.multiple_of((row // 8) * 8, 8), 8)
            out_ref[at, :] += jnp.where(sub == lax.rem(row, 8), taken, 0.0)
            return carry

        lax.fori_loop(off_dup_ref[k, blk], off_dup_ref[k, blk + 1], dup_step, 0)


def table_grad(vocab_local, off_one, off_dup, dup_ids, one_ids, ones, dups, prev=None):
    n_peer, dim = len(ones), ones[0].shape[1]
    n_blk = pl.cdiv(vocab_local, V_BLOCK)
    smem = pl.BlockSpec(memory_space=pltpu.SMEM)
    whole = pl.BlockSpec(memory_space=pltpu.VMEM)
    rows = pl.BlockSpec((V_BLOCK, dim), lambda b: (b, 0))
    extra = () if prev is None else (prev,)
    return pl.pallas_call(
        functools.partial(table_kernel, n_peer=n_peer, has_prev=prev is not None),
        grid=(n_blk,),
        out_shape=jax.ShapeDtypeStruct((vocab_local, dim), F32),
        in_specs=[smem, smem, smem, whole] + [whole] * (2 * n_peer) + [rows] * len(extra),
        out_specs=rows,
        scratch_shapes=[
            pltpu.VMEM((n_peer * WIN, dim), BF16),
            pltpu.VMEM((n_peer * WIN, 1), jnp.int32),
        ],
        input_output_aliases={} if prev is None else {4 + 2 * n_peer: 0},
        cost_estimate=pl.CostEstimate(flops=25 * 10 ** 9, bytes_accessed=75 * 10 ** 6, transcendentals=0),
        name='table_grad',
    )(off_one, off_dup, dup_ids, one_ids, *ones, *dups, *extra)


def solution(mesh):
    tok_spec = P(('data', 'tensor'))
    row_spec = P(('data', 'tensor'), None)
    n_peer = mesh.shape['tensor']
    swaps = [[(i, i ^ k) for i in range(n_peer)] for k in range(n_peer)]

    def exchange(k, block):
        return block if k == 0 else lax.ppermute(block, 'tensor', swaps[k])

    def local_step(token_ids, emb_shard, norm_gain, w_up, w_down, grad_out):
        vocab_local = emb_shard.shape[0]
        n_tok = token_ids.shape[0]
        me = lax.axis_index('tensor')
        peers = me ^ jnp.arange(n_peer, dtype=jnp.int32)
        w_dn = lax.all_gather(w_down, 'tensor', tiled=True)
        w_up_t = lax.all_gather(w_up.T, 'tensor', tiled=True)

        sorted_ids = jnp.sort(token_ids).reshape(n_tok // 128, 128)
        rows_of = slice(0, N_REQ // 128)

        def asked(rnd):
            mine = route(me, jnp.int32(rnd), sorted_ids, n_peer, vocab_local)
            if isinstance(rnd, int):
                theirs = swap_lists(mine)
            else:
                theirs = jnp.stack([exchange(k, mine[k]) for k in range(n_peer)])
            rounds = jnp.max(theirs[:, -1, :])
            mine, theirs = (part[:, rows_of, :].reshape(n_peer, N_REQ) for part in (mine, theirs))
            return mine, jnp.where(theirs < 0, -1, theirs - me * vocab_local), rounds

        first = asked(0)
        rounds = first[2]
        halves = (range(n_peer // 2, n_peer), range(n_peer // 2))
        ids_col, ids_row = token_ids[:, None], token_ids[None, :]
        gain_row = norm_gain[None, :]

        def lookup(lists, prev=None):
            mine, theirs, _ = lists
            idx = jnp.clip(theirs, 0, vocab_local - 1)
            recv = {}
            for half in halves:
                blocks = gather_rows(emb_shard, idx[half.start:half.stop].reshape(-1), len(half))
                recv.update({k: exchange(k, block) for k, block in zip(half, blocks)})
            return expand_rows(ids_col, mine, gain_row, [recv[k] for k in range(n_peer)], prev)

        def lookup_step(carry):
            rnd, x_prev, _ = carry
            x_new, n_new = lookup(asked(rnd), x_prev)
            return rnd + 1, x_new, n_new

        x_first, n_first = lookup(first)
        _, x_local, normed = lax.while_loop(lambda c: c[0] < rounds, lookup_step, (jnp.int32(1), x_first, n_first))

        x_f = x_local.astype(F32)
        gain_f = norm_gain.astype(F32)
        _, norm_back = jax.vjp(lambda x_in: rms_norm(x_in, gain_f), x_f)
        hidden, d_pre = hidden_arrays(normed, grad_out, w_up_t, w_dn)
        d_w_down = lax.psum_scatter(contract_first(hidden, grad_out), 'tensor', scatter_dimension=0, tiled=True)
        d_norm = matmul(d_pre, w_up_t)
        dx_local = (grad_out.astype(F32) + norm_back(d_norm)[0]).astype(BF16)
        d_w_up = lax.psum_scatter(contract_first(d_pre, normed), 'tensor', scatter_dimension=0, tiled=True).T
        out_local = (x_f + matmul(hidden, w_dn)).astype(BF16)

        def table(lists, prev=None):
            mine, theirs, _ = lists
            dups, ones = {}, {}
            for half in halves:
                gid_col = mine[half.start:half.stop].reshape(-1, 1)
                for k, dup, one in zip(half, *combine_rows(gid_col, ids_row, dx_local)):
                    ones[k], dups[k] = exchange(k, one), exchange(k, dup)
            ones, dups = ([part[k] for k in range(n_peer)] for part in (ones, dups))
            keys = jnp.where(theirs < 0, BIG, theirs)
            marks = jnp.arange(pl.cdiv(vocab_local, V_BLOCK) + 1, dtype=jnp.int32) * V_BLOCK
            offs = [jnp.sum(part[:, None, :] < marks[None, :, None], axis=-1, dtype=jnp.int32)
                    for part in (keys[:, :N_DUP], keys[:, N_DUP:])]
            return table_grad(vocab_local, offs[1], offs[0], theirs[:, :N_DUP],
                              theirs[:, N_DUP:].reshape(n_peer * N_ONE, 1), ones, dups, prev)

        def table_step(carry):
            rnd, prev = carry
            return rnd + 1, table(asked(rnd), prev)

        _, d_emb = lax.while_loop(lambda c: c[0] < rounds, table_step, (jnp.int32(1), table(first)))
        return out_local, d_emb, d_w_up, d_w_down

    return jax.shard_map(
        local_step,
        mesh=mesh,
        in_specs=(tok_spec, P('tensor', None), P(None), P(None, 'tensor'), P('tensor', None), row_spec),
        out_specs=(row_spec, row_spec, P('data', 'tensor'), row_spec),
        check_vma=False,
    )
```

time: 3090 us -> 690 us (0.22)
  local copies, waits for them, and re-layouts: 1520 us -> 12.4 us
  other arithmetic: 685 us -> 27 us
  waiting for transfers between devices: 458 us -> 68.7 us
  Pallas kernels: 0 us -> 324 us
  matrix products: 382 us -> 207 us
    gather x1 -> x0, local copies, waits for them, and re-layouts: 1470 us -> none  [local_step(): jnp.take(emb_shard, jnp.clip(rel_ids, 0, vocab_local - 1), axis=0)]
    scatter-add x3 -> x0, other arithmetic: 571 us -> none  [local_step(): jax.ops.segment_sum(dx_all.astype(jnp.float32), seg_ids, num_segments=voc...]
    unnamed x7 -> x4, waiting for transfers between devices: 351 us -> 0.73 us
    pallas_call x0 -> x9, Pallas kernels: none -> 324 us  [the longest x1 123 us: hidden_arrays(): pl.pallas_call(hidden_kernel, grid=(n_tok // TOK_BLOCK,), out_shape=[jax....]
    dot_general x4 -> x2, matrix products: 247 us -> 101 us  [matmul(): return jnp.dot(left_op, right_op, preferred_element_type=F32)]
    ppermute x0 -> x21, waiting for transfers between devices: none -> 67.9 us  [exchange(): return block if k == 0 else lax.ppermute(block, 'tensor', swaps[k])]
    all_gather x1 -> x0, waiting for transfers between devices: 58.3 us -> none  [local_step(): dx_all = lax.all_gather(dx_local, 'tensor', tiled=True)]
    convert_element_type x3 -> x2, other arithmetic: 69.2 us -> 11.9 us  [the longest x1 11.9 us: local_step(): dx_local = (grad_out.astype(F32) + norm_back(d_norm)[0]).astype(BF16)]
  transfers between devices with their start and end apart: 6 -> 25, of which waited for: 4 -> 5; matrix products, arithmetic and copies ran while one was open for 30% -> 28% of each run, Pallas kernels for 0% -> 30%
where the time goes in v2:
time: 690 us; the launch traced here: 678 us
  Pallas kernels  324 us (47%)
  matrix products  207 us (30%)
  waiting for transfers between devices  68.7 us (10%)
  other arithmetic  27 us (4%)
  starting transfers between devices  21.9 us (3%)
  between operations  14.4 us (2%)
  local copies, waits for them, and re-layouts  12.4 us (2%)
    pallas_call x1, Pallas kernels, hidden_arrays(): pl.pallas_call(hidden_kernel, grid=(n_tok // TOK_BLOCK,), out_shape=[jax....  123 us
    dot_general x2, matrix products, contract_first(): lax.dot_general(left_op, right_op, (((0,), (0,)), ((), ())), preferred_el...  106 us
    dot_general x2, matrix products, matmul(): return jnp.dot(left_op, right_op, preferred_element_type=F32)  101 us
    ppermute x21, waiting for transfers between devices, exchange(): return block if k == 0 else lax.ppermute(block, 'tensor', swaps[k])  67.9 us
    pallas_call x1, Pallas kernels, table_grad(): pl.pallas_call(functools.partial(table_kernel, n_peer=n_peer, has_prev=pr...  61.5 us
    pallas_call x2, Pallas kernels, gather_rows(): pl.pallas_call(functools.partial(gather_kernel, n_out=n_out, depth=depth)...  59 us
    pallas_call x2, Pallas kernels, combine_rows(): pl.pallas_call(functools.partial(combine_kernel, n_out=n_out), out_shape=...  35 us
    pallas_call x1, Pallas kernels, expand_rows(): pl.pallas_call(functools.partial(expand_kernel, n_peer=n_peer, has_prev=p...  33.8 us
  transfers between devices with their start and end apart: 25, of which 5 were waited for; matrix products, arithmetic and copies ran while one was open for 28% of the time, Pallas kernels for 30%

profile of v2, /device:TPU:0, one launch (start us, length us, event | category | flops | bytes accessed | tf_op | source)
XLA Modules:
  0.0 677.6 jit_solution(12012603255757919715)
XLA Ops:
  8.0 6.5 sort.15
  14.5 3.0 route.8.mine_ref
  17.4 8.3 %swap_lists.1 = s32[8,8,128]{2,1,0:T(8,128)} custom-call(s32[8,8,128]{2,1,0:T(8,128)} %route.8.mine_ref), custom_call_target="tpu_custom_call" | custom-call | tf_op jit(solution)/shard_map/swap_lists/pallas_call | solution.py:139
  29.8 29.0 %gather_rows.13 = (bf16[384,896]{1,0:T(8,128)(2,1)}, bf16[384,896]{1,0:T(8,128)(2,1)}, bf16[384,896]{1,0:T(8,128)(2,1)}, bf16[384,896]{1,0:T(8,128)(2,1)}) custom-call(s32[1536]{0:T(1024)} %fusion.19.idx_ref, s32[1536,1]{1,0:T(8,128)} %add_select_fusion.4.sub_ref, bf16[18992,896]{1,0:T(8,128)(2,1)} %emb_ref.3), custom_call_target="tpu_custom_call" | custom-call | flops 14000000000 | bytes 22020096 | tf_op jit(solution)/shard_map/gather_rows/pallas_call | solution.py:188
  58.9 3.1 collective-permute-start.38
  62.2 2.1 collective-permute-start.41
  66.4 30.0 %gather_rows.12 = (bf16[384,896]{1,0:T(8,128)(2,1)}, bf16[384,896]{1,0:T(8,128)(2,1)}, bf16[384,896]{1,0:T(8,128)(2,1)}, bf16[384,896]{1,0:T(8,128)(2,1)}) custom-call(s32[1536]{0:T(1024)} %fusion.17.idx_ref, s32[1536,1]{1,0:T(8,128)} %add_select_fusion.5.sub_ref, bf16[18992,896]{1,0:T(8,128)(2,1)} %emb_ref.3), custom_call_target="tpu_custom_call" | custom-call | flops 14000000000 | bytes 22020096 | tf_op jit(solution)/shard_map/gather_rows/pallas_call | solution.py:188
  96.5 11.0 %collective-permute-done.38.refs_4_ = bf16[384,896]{1,0:T(8,128)(2,1)S(1)} collective-permute-done((bf16[384,896]{1,0:T(8,128)(2,1)}, bf16[384,896]{1,0:T(8,128)(2,1)S(1)}, u32[]{:S(2)}, u32[]{:S(2)}) %collective-permute-start.38) | collective-permute-done | bytes 688160 | tf_op jit(solution)/shard_map/ppermute | solution.py:394
  107.9 12.2 %collective-permute-done.39.refs_5_ = bf16[384,896]{1,0:T(8,128)(2,1)S(1)} collective-permute-done((bf16[384,896]{1,0:T(8,128)(2,1)}, bf16[384,896]{1,0:T(8,128)(2,1)S(1)}, u32[]{:S(2)}, u32[]{:S(2)}) %collective-permute-start.39) | collective-permute-done | bytes 688160 | tf_op jit(solution)/shard_map/ppermute | solution.py:394
  120.1 2.2 collective-permute-start.37
  125.9 21.3 %collective-permute-done.37.refs_3_ = bf16[384,896]{1,0:T(8,128)(2,1)} collective-permute-done((bf16[384,896]{1,0:T(8,128)(2,1)}, bf16[384,896]{1,0:T(8,128)(2,1)}, u32[]{:S(2)}, u32[]{:S(2)}) %collective-permute-start.37) | collective-permute-done | bytes 688160 | tf_op jit(solution)/shard_map/ppermute | solution.py:394
  147.2 33.8 %expand_rows.6 = (bf16[4096,896]{1,0:T(8,128)(2,1)}, bf16[4096,896]{1,0:T(8,128)(2,1)}) custom-call(s32[4096,1]{1,0:T(8,128)S(1)} %copy.70.ids_ref, s32[8,384]{1,0:T(8,128)} %bitcast.162, bf16[1,896]{1,0:T(2,128)(2,1)S(1)} %broadcast_in_dim.50.gain_ref, bf16[384,896]{1,0:T(8,128)(2,1)} %get-tuple-element.283.refs_0_, ...), custom_call_target="tpu_custom_call" | custom-call | flops 22000001024 | bytes 30000000 | tf_op jit(solution)/shard_map/expand_rows/pallas_call | solution.py:227
  181.9 123.2 %hidden_arrays.1 = (bf16[4096,4864]{1,0:T(8,128)(2,1)}, bf16[4096,4864]{1,0:T(8,128)(2,1)}) custom-call(bf16[4096,896]{1,0:T(8,128)(2,1)} %get-tuple-element.294.n_ref, bf16[4096,896]{1,0:T(8,128)(2,1)} %grad_ref.1, bf16[4864,896]{1,0:T(8,128)(2,1)} %all-gather.3.cloned.1.call-done.w_up_ref, bf16[4864,896]{1,0:T(8,128)(2,1)} %all-gather.5.cloned.1.call-done.w_dn_ref), custom_call_target="tpu_custom_call" | custom-call | flops 71403831296 | bytes 110000000 | tf_op jit(solution)/shard_map/hidden_arrays/pallas_call | solution.py:277
  305.1 53.2 %fusion.26 = f32[4864,896]{1,0:T(8,128)} fusion(bf16[4096,4864]{1,0:T(8,128)(2,1)} %get-tuple-element.295, bf16[4096,896]{1,0:T(8,128)(2,1)} %grad_ref.1), kind=kOutput, calls=%fused_computation.116 | convolution fusion | flops 35701915648 | bytes 64618496 | tf_op jit(solution)/shard_map/dot_general | solution.py:37
  367.3 51.6 %fusion.11 = (f32[4096]{0:T(1024)S(1)}, f32[4096]{0:T(1024)S(1)}, f32[4096,896]{1,0:T(8,128)}) fusion(bf16[4096,896]{1,0:T(8,128)(2,1)} %get-tuple-element.293, f32[896]{0:T(1024)S(1)} %convert_element_type.34, bf16[4096,4864]{1,0:T(8,128)(2,1)} %get-tuple-element.296, bf16[4864,896]{1,0:T(8,128)(2,1)} %all-gather.3.cloned.1.call-done.w_up_ref), kind=kOutput, calls=%fused_computation.71 | convolution fusion | flops 35723927552 | bytes 70618624 | tf_op jit(solution)/shard_map/dot_general | solution.py:41
  419.0 11.9 %fusion.9.dx_ref = bf16[4096,896]{1,0:T(8,128)(2,1)} fusion(bf16[4096,896]{1,0:T(8,128)(2,1)S(1)} %bitcast.157, bf16[4096,896]{1,0:T(8,128)(2,1)} %grad_ref.1, f32[4096,896]{1,0:T(8,128)} %get-tuple-element.414, f32[4096]{0:T(1024)S(1)} %get-tuple-element.409, f32[4096]{0:T(1024)S(1)} %get-tuple-element.408, f32[896]{0:T(1024)S(1)} %convert_element_type.34), kind=kLoop, calls=%fused_computation.69 | loop fusion | flops 33030144 | bytes 36736512 | tf_op jit(solution)/shard_map/convert_element_type | solution.py:446
  430.8 17.5 %combine_rows.7 = (f32[48,896]{1,0:T(8,128)}, f32[48,896]{1,0:T(8,128)}, f32[48,896]{1,0:T(8,128)}, f32[48,896]{1,0:T(8,128)}, bf16[336,896]{1,0:T(8,128)(2,1)},...) custom-call(s32[1536,1]{1,0:T(8,128)} %reshape.368.gid_ref, ...), custom_call_target="tpu_custom_call" | custom-call | flops 12000000000 | bytes 12000000 | tf_op jit(solution)/shard_map/combine_rows/pallas_call | solution.py:307
  449.3 2.8 collective-permute-start.54
  452.7 17.5 %combine_rows.6 = (f32[48,896]{1,0:T(8,128)}, f32[48,896]{1,0:T(8,128)}, f32[48,896]{1,0:T(8,128)}, f32[48,896]{1,0:T(8,128)}, bf16[336,896]{1,0:T(8,128)(2,1)},...) custom-call(s32[1536,1]{1,0:T(8,128)} %reshape.367.gid_ref, ...), custom_call_target="tpu_custom_call" | custom-call | flops 12000000000 | bytes 12000000 | tf_op jit(solution)/shard_map/combine_rows/pallas_call | solution.py:307
  472.2 1.9 collective-permute-start.49
  476.4 53.2 %fusion.25 = f32[4864,896]{1,0:T(8,128)} fusion(bf16[4096,4864]{1,0:T(8,128)(2,1)} %get-tuple-element.296, bf16[4096,896]{1,0:T(8,128)(2,1)} %get-tuple-element.294.n_ref), kind=kOutput, calls=%fused_computation.115 | convolution fusion | flops 35701915648 | bytes 64618496 | tf_op jit(solution)/shard_map/dot_general | solution.py:37
  535.3 48.9 %fusion.10 = bf16[4096,896]{1,0:T(8,128)(2,1)} fusion(bf16[4096,896]{1,0:T(8,128)(2,1)} %get-tuple-element.293, bf16[4096,4864]{1,0:T(8,128)(2,1)} %get-tuple-element.295, bf16[4864,896]{1,0:T(8,128)(2,1)} %all-gather.5.cloned.1.call-done.w_dn_ref), kind=kOutput, calls=%fused_computation.70 | convolution fusion | flops 35712925696 | bytes 63242240 | tf_op jit(solution)/shard_map/dot_general | solution.py:41
  584.3 22.4 %collective-permute-done.44.refs_3_ = bf16[336,896]{1,0:T(8,128)(2,1)S(1)} collective-permute-done((bf16[336,896]{1,0:T(8,128)(2,1)S(1)}, bf16[336,896]{1,0:T(8,128)(2,1)S(1)}, u32[]{:S(2)}, u32[]{:S(2)}) %collective-permute-start.44) | collective-permute-done | bytes 602144 | tf_op jit(solution)/shard_map/ppermute | solution.py:394
  607.6 61.5 %table_grad.3 = f32[18992,896]{1,0:T(8,128)} custom-call(s32[8,76]{1,0:T(8,128)} %copy.75.off_one_ref, s32[8,76]{1,0:T(8,128)} %convert_reduce_fusion.3.off_dup_ref, s32[8,48]{1,0:T(8,128)} %slice.230.dup_id_ref, s32[2688,1]{1,0:T(8,128)} %reshape.366.one_id_ref, bf16[336,896]{1,0:T(8,128)(2,1)} %get-tuple-element.297.refs_0_, bf16[336,896]{1,0:T(8,128)(2,1)} %copy-done.36, ...), custom_call_target="tpu_custom_call" | custom-call | flops 24999999488 | bytes 75000000 | tf_op jit(solution)/shard_map/table_grad/pallas_call | solution.py:371
  (138 shorter events, 35.0 us)
Async XLA Ops:
  7.2 174.7 %all-gather.3.cloned.1.call-start = ((), (), s32[]{:S(2)}) async-start(), calls=%async_computation.2 | async-start | bytes 9805824 | tf_op jit(solution)/shard_map/all_gather | solution.py:402
  7.9 174.0 %all-gather.5.cloned.1.call-start = ((), (), s32[]{:S(2)}) async-start(), calls=%async_computation.3 | async-start | bytes 9805824 | tf_op jit(solution)/shard_map/all_gather | solution.py:401
  58.9 48.7 %collective-permute-start.38 = (bf16[384,896]{1,0:T(8,128)(2,1)}, bf16[384,896]{1,0:T(8,128)(2,1)S(1)}, u32[]{:S(2)}, u32[]{:S(2)}) collective-permute-start(bf16[384,896]{1,0:T(8,128)(2,1)} %get-tuple-element.287), channel_id=1, source_target_pairs={{0,4},{1,5},{2,6},{3,7},{4,0},{5,1},{6,2},{7,3}} | collective-permute-start | bytes 2064392 | tf_op jit(solution)/shard_map/ppermute | solution.py:394
  61.9 58.2 %collective-permute-start.39 = (bf16[384,896]{1,0:T(8,128)(2,1)}, bf16[384,896]{1,0:T(8,128)(2,1)S(1)}, u32[]{:S(2)}, u32[]{:S(2)}) collective-permute-start(bf16[384,896]{1,0:T(8,128)(2,1)} %get-tuple-element.288), channel_id=1, source_target_pairs={{0,5},{1,4},{2,7},{3,6},{4,1},{5,0},{6,3},{7,2}} | collective-permute-start | bytes 2064392 | tf_op jit(solution)/shard_map/ppermute | solution.py:394
  61.9 63.9 %collective-permute-start.40 = (bf16[384,896]{1,0:T(8,128)(2,1)}, bf16[384,896]{1,0:T(8,128)(2,1)}, u32[]{:S(2)}, u32[]{:S(2)}) collective-permute-start(bf16[384,896]{1,0:T(8,128)(2,1)} %get-tuple-element.289), channel_id=1, source_target_pairs={{0,6},{1,7},{2,4},{3,5},{4,2},{5,3},{6,0},{7,1}} | collective-permute-start | bytes 2064392 | tf_op jit(solution)/shard_map/ppermute | solution.py:394
  62.2 63.6 %collective-permute-start.41 = (bf16[384,896]{1,0:T(8,128)(2,1)}, bf16[384,896]{1,0:T(8,128)(2,1)}, u32[]{:S(2)}, u32[]{:S(2)}) collective-permute-start(bf16[384,896]{1,0:T(8,128)(2,1)} %get-tuple-element.290), channel_id=1, source_target_pairs={{0,7},{1,6},{2,5},{3,4},{4,3},{5,2},{6,1},{7,0}} | collective-permute-start | bytes 2064392 | tf_op jit(solution)/shard_map/ppermute | solution.py:394
  96.4 29.4 %collective-permute-start.35 = (bf16[384,896]{1,0:T(8,128)(2,1)}, bf16[384,896]{1,0:T(8,128)(2,1)}, u32[]{:S(2)}, u32[]{:S(2)}) collective-permute-start(bf16[384,896]{1,0:T(8,128)(2,1)} %get-tuple-element.284), channel_id=1, source_target_pairs={{0,1},{1,0},{2,3},{3,2},{4,5},{5,4},{6,7},{7,6}} | collective-permute-start | bytes 2064392 | tf_op jit(solution)/shard_map/ppermute | solution.py:394
  120.1 27.1 %collective-permute-start.37 = (bf16[384,896]{1,0:T(8,128)(2,1)}, bf16[384,896]{1,0:T(8,128)(2,1)}, u32[]{:S(2)}, u32[]{:S(2)}) collective-permute-start(bf16[384,896]{1,0:T(8,128)(2,1)} %get-tuple-element.286), channel_id=1, source_target_pairs={{0,3},{1,2},{2,1},{3,0},{4,7},{5,6},{6,5},{7,4}} | collective-permute-start | bytes 2064392 | tf_op jit(solution)/shard_map/ppermute | solution.py:394
  122.3 548.5 %reduce-scatter.5.cloned.1.call-start = ((), (), s32[]{:S(2)}) async-start(), calls=%async_computation.5 | async-start | bytes 19611648 | tf_op jit(solution)/shard_map/reduce_scatter | solution.py:444
  358.4 312.5 %reduce-scatter.3.cloned.1.call-start = ((), (), s32[]{:S(2)}) async-start(), calls=%async_computation.4 | async-start | bytes 19611648 | tf_op jit(solution)/shard_map/reduce_scatter | solution.py:447
  448.3 23.1 %collective-permute-start.52 = (f32[48,896]{1,0:T(8,128)}, f32[48,896]{1,0:T(8,128)S(1)}, u32[]{:S(2)}, u32[]{:S(2)}) collective-permute-start(f32[48,896]{1,0:T(8,128)} %get-tuple-element.309), channel_id=1, source_target_pairs={{0,4},{1,5},{2,6},{3,7},{4,0},{5,1},{6,2},{7,3}} | collective-permute-start | bytes 516104 | tf_op jit(solution)/shard_map/ppermute | solution.py:394
  448.4 23.9 %collective-permute-start.53 = (f32[48,896]{1,0:T(8,128)}, f32[48,896]{1,0:T(8,128)S(1)}, u32[]{:S(2)}, u32[]{:S(2)}) collective-permute-start(f32[48,896]{1,0:T(8,128)} %get-tuple-element.310), channel_id=1, source_target_pairs={{0,5},{1,4},{2,7},{3,6},{4,1},{5,0},{6,3},{7,2}} | collective-permute-start | bytes 516104 | tf_op jit(solution)/shard_map/ppermute | solution.py:394
  449.3 24.8 %collective-permute-start.54 = (f32[48,896]{1,0:T(8,128)}, f32[48,896]{1,0:T(8,128)S(1)}, u32[]{:S(2)}, u32[]{:S(2)}) collective-permute-start(f32[48,896]{1,0:T(8,128)} %get-tuple-element.311), channel_id=1, source_target_pairs={{0,6},{1,7},{2,4},{3,5},{4,2},{5,3},{6,0},{7,1}} | collective-permute-start | bytes 516104 | tf_op jit(solution)/shard_map/ppermute | solution.py:394
  452.1 23.6 %collective-permute-start.55 = (f32[48,896]{1,0:T(8,128)}, f32[48,896]{1,0:T(8,128)S(1)}, u32[]{:S(2)}, u32[]{:S(2)}) collective-permute-start(f32[48,896]{1,0:T(8,128)} %get-tuple-element.312), channel_id=1, source_target_pairs={{0,7},{1,6},{2,5},{3,4},{4,3},{5,2},{6,1},{7,0}} | collective-permute-start | bytes 516104 | tf_op jit(solution)/shard_map/ppermute | solution.py:394
  470.3 63.6 %collective-permute-start.45 = (bf16[336,896]{1,0:T(8,128)(2,1)}, bf16[336,896]{1,0:T(8,128)(2,1)S(1)}, u32[]{:S(2)}, u32[]{:S(2)}) collective-permute-start(bf16[336,896]{1,0:T(8,128)(2,1)} %get-tuple-element.301), channel_id=1, source_target_pairs={{0,4},{1,5},{2,6},{3,7},{4,0},{5,1},{6,2},{7,3}} | collective-permute-start | bytes 1806344 | tf_op jit(solution)/shard_map/ppermute | solution.py:394
  471.4 63.6 %collective-permute-start.46 = (bf16[336,896]{1,0:T(8,128)(2,1)}, bf16[336,896]{1,0:T(8,128)(2,1)S(1)}, u32[]{:S(2)}, u32[]{:S(2)}) collective-permute-start(bf16[336,896]{1,0:T(8,128)(2,1)} %get-tuple-element.302), channel_id=1, source_target_pairs={{0,5},{1,4},{2,7},{3,6},{4,1},{5,0},{6,3},{7,2}} | collective-permute-start | bytes 1806344 | tf_op jit(solution)/shard_map/ppermute | solution.py:394
  472.2 57.5 %collective-permute-start.49 = (f32[48,896]{1,0:T(8,128)}, f32[48,896]{1,0:T(8,128)S(1)}, u32[]{:S(2)}, u32[]{:S(2)}) collective-permute-start(f32[48,896]{1,0:T(8,128)} %get-tuple-element.306), channel_id=1, source_target_pairs={{0,1},{1,0},{2,3},{3,2},{4,5},{5,4},{6,7},{7,6}} | collective-permute-start | bytes 516104 | tf_op jit(solution)/shard_map/ppermute | solution.py:394
  474.2 57.2 %collective-permute-start.50 = (f32[48,896]{1,0:T(8,128)}, f32[48,896]{1,0:T(8,128)S(1)}, u32[]{:S(2)}, u32[]{:S(2)}) collective-permute-start(f32[48,896]{1,0:T(8,128)} %get-tuple-element.307), channel_id=1, source_target_pairs={{0,2},{1,3},{2,0},{3,1},{4,6},{5,7},{6,4},{7,5}} | collective-permute-start | bytes 516104 | tf_op jit(solution)/shard_map/ppermute | solution.py:394
  475.8 57.5 %collective-permute-start.51 = (f32[48,896]{1,0:T(8,128)}, f32[48,896]{1,0:T(8,128)S(1)}, u32[]{:S(2)}, u32[]{:S(2)}) collective-permute-start(f32[48,896]{1,0:T(8,128)} %get-tuple-element.308), channel_id=1, source_target_pairs={{0,3},{1,2},{2,1},{3,0},{4,7},{5,6},{6,5},{7,4}} | collective-permute-start | bytes 516104 | tf_op jit(solution)/shard_map/ppermute | solution.py:394
  530.8 53.4 %collective-permute-start.47 = (bf16[336,896]{1,0:T(8,128)(2,1)S(1)}, bf16[336,896]{1,0:T(8,128)(2,1)S(1)}, u32[]{:S(2)}, u32[]{:S(2)}) collective-permute-start(bf16[336,896]{1,0:T(8,128)(2,1)S(1)} %copy-done.30), channel_id=1, source_target_pairs={{0,6},{1,7},{2,4},{3,5},{4,2},{5,3},{6,0},{7,1}} | collective-permute-start | bytes 1806344 | tf_op jit(solution)/shard_map/ppermute | solution.py:394
  531.3 52.9 %collective-permute-start.48 = (bf16[336,896]{1,0:T(8,128)(2,1)S(1)}, bf16[336,896]{1,0:T(8,128)(2,1)S(1)}, u32[]{:S(2)}, u32[]{:S(2)}) collective-permute-start(bf16[336,896]{1,0:T(8,128)(2,1)S(1)} %copy-done.29), channel_id=1, source_target_pairs={{0,7},{1,6},{2,5},{3,4},{4,3},{5,2},{6,1},{7,0}} | collective-permute-start | bytes 1806344 | tf_op jit(solution)/shard_map/ppermute | solution.py:394
  533.2 51.0 %collective-permute-start.42 = (bf16[336,896]{1,0:T(8,128)(2,1)}, bf16[336,896]{1,0:T(8,128)(2,1)S(1)}, u32[]{:S(2)}, u32[]{:S(2)}) collective-permute-start(bf16[336,896]{1,0:T(8,128)(2,1)} %get-tuple-element.298), channel_id=1, source_target_pairs={{0,1},{1,0},{2,3},{3,2},{4,5},{5,4},{6,7},{7,6}} | collective-permute-start | bytes 1806344 | tf_op jit(solution)/shard_map/ppermute | solution.py:394
  533.9 50.4 %collective-permute-start.43 = (bf16[336,896]{1,0:T(8,128)(2,1)}, bf16[336,896]{1,0:T(8,128)(2,1)S(1)}, u32[]{:S(2)}, u32[]{:S(2)}) collective-permute-start(bf16[336,896]{1,0:T(8,128)(2,1)} %get-tuple-element.299), channel_id=1, source_target_pairs={{0,2},{1,3},{2,0},{3,1},{4,6},{5,7},{6,4},{7,5}} | collective-permute-start | bytes 1806344 | tf_op jit(solution)/shard_map/ppermute | solution.py:394
  535.1 71.7 %collective-permute-start.44 = (bf16[336,896]{1,0:T(8,128)(2,1)S(1)}, bf16[336,896]{1,0:T(8,128)(2,1)S(1)}, u32[]{:S(2)}, u32[]{:S(2)}) collective-permute-start(bf16[336,896]{1,0:T(8,128)(2,1)S(1)} %copy-done.33), channel_id=1, source_target_pairs={{0,3},{1,2},{2,1},{3,0},{4,7},{5,6},{6,5},{7,4}} | collective-permute-start | bytes 1806344 | tf_op jit(solution)/shard_map/ppermute | solution.py:394
  (29 other events, 683.0 us)
Sparse Core Ops, SparseCore 0:
  9.8 53.1 all-gather.2
  122.5 57.7 all-gather.4
  358.5 136.0 reduce-scatter.4
  529.8 133.5 reduce-scatter.2
